TPU v7x, 256 devices: a whole 4x4x8 slice. The times are simulated.
256 devices in a mesh: box: 16 (over y_lo, z), dir: 16 (over x, y_hi, core).
Axes of the slice: x: 4, y: 4 (y_hi: 2, y_lo: 2; y = y_hi * 2 + y_lo), z: 8, core: 2. Of those that a mesh axis runs over, the one named last changes fastest.
Arguments:
- sources: float32 [2, 4, 96, 96, 128], P(None, None, 'box', 'dir'), may hold values from -6 to 6
- radiation: float32 [2, 512, 128], replicated, may hold values from -0.5 to 0.5
- interp: float32 [1024, 512], replicated, may hold values from -0.25 to 0.25
- trans_fine: float32 [2, 49, 512], replicated, may hold values from -1.2 to 1.2
- trans_coarse: float32 [2, 49, 1024], replicated, may hold values from -1.2 to 1.2
- child_phase: float32 [4, 1024], replicated, may hold values from -3.140625 to 3.140625
- near_block: float32 [2, 9, 128, 128], replicated, may hold values from -0.5 to 0.5
- far_fine: int32 [96, 96, 49], P('box', 'dir'), may hold values from 0 to 1, as said below
- far_coarse: int32 [48, 48, 49], P('box'), may hold values from 0 to 1, as said below
- near_mask: int32 [96, 96, 9], P('box', 'dir'), may hold values from 0 to 1, as said below
Outputs:
- product: float32 [2, 4, 96, 96, 128], P(None, None, 'box', 'dir')
Inputs may be any that keep to these rules, and one draw needn't show every extreme that they name: `far_fine`: flags of displacements within one box (the centre 3 x 3) are 0. `far_coarse`: flags of displacements within one box (the centre 3 x 3) are 0. `near_mask`: the flag of the box itself (index 4) is 1.
All inputs are finite; a program needn't handle non-finite values.
Results may differ from a plain program's by a relative error of at most 0.0001.
Values sent between devices are 32-bit elements; how exact they have to be, the bound alone decides.
A program may use at most 128 MiB of HBM per device.

v0:
```python
import math

import jax
import jax.numpy as jnp
from jax import lax
from jax.experimental import pallas as pl
from jax.experimental.pallas import tpu as pltpu
from jax.sharding import PartitionSpec as P

OUTER = [o for o in range(49) if max(abs(o // 7 - 3), abs(o % 7 - 3)) > 1]
F32 = jnp.float32
BF16 = jnp.bfloat16
NN = (((1,), (0,)), ((), ()))
NT = (((1,), (1,)), ((), ()))


def split(x):
    high = x.astype(BF16)
    return high, (x - high.astype(F32)).astype(BF16)


def dot3(a, b, dims):
    a_high, a_low = a
    b_high, b_low = b
    return (
        lax.dot_general(a_high, b_high, dims, preferred_element_type=F32)
        + lax.dot_general(a_low, b_high, dims, preferred_element_type=F32)
        + lax.dot_general(a_high, b_low, dims, preferred_element_type=F32)
    )


def turn(v):
    axis = v.ndim - 2
    rows = lax.broadcasted_iota(jnp.int32, v.shape, axis)
    return jnp.where(rows < 4, -1.0, 1.0) * pltpu.roll(v, 4, axis)


def weights(rad_ref, interp_ref, rad_h, rad_l, wide_h, wide_l):
    for plane in range(2):
        high, low = split(rad_ref[plane])
        rad_h[:, plane * 128 : (plane + 1) * 128] = high
        rad_l[:, plane * 128 : (plane + 1) * 128] = low

    def some(step, _):
        rows = pl.ds(pl.multiple_of(step * 256, 256), 256)
        value = dot3(split(interp_ref[rows, :]), (rad_h[...], rad_l[...]), NN)
        high, low = split(value)
        wide_h[rows, :] = high
        wide_l[rows, :] = low
        return 0

    lax.fori_loop(0, 4, some, 0)


def tables(tf_ref, tc_ref, ff_ref, fc_ref, nm_ref, fine_g, coarse_g, near_g, listed, first):
    for row in range(3):
        for col in range(3):
            listed[3 * row + col : 3 * row + col + 1, 0:49] = fc_ref[
                row, pl.ds(first + col, 1), :
            ].astype(F32)
    flags_c = listed[0:9, 0:49]
    for at, o in enumerate(OUTER):
        flag = jnp.broadcast_to(flags_c[:, o : o + 1], (9, 128))
        for plane in range(2):
            for mt in range(8):
                coarse_g[plane, mt, at * 16 : at * 16 + 9, :] = (
                    flag * tc_ref[o, plane : plane + 1, mt * 128 : (mt + 1) * 128]
                )
    for x in range(6):
        flags = ff_ref[x].astype(F32)
        for at, o in enumerate(OUTER):
            flag = jnp.broadcast_to(flags[:, o : o + 1], (6, 128))
            base = (at * 3 + x % 3) * 8
            for plane in range(2):
                for kt in range(4):
                    fine_g[plane, kt, x // 3, base : base + 6, :] = (
                        flag * tf_ref[o, plane : plane + 1, kt * 128 : (kt + 1) * 128]
                    )
        near = nm_ref[x].astype(F32)
        for o in range(9):
            near_g[o, x, 0:6, :] = jnp.broadcast_to(near[:, o : o + 1], (6, 128))


def arrange(tiles, row, boxes_a, boxes_h, boxes_l):
    def one(x, _):
        parts = []
        for col in range(3):
            re = tiles[row, col, 0, x]
            im = tiles[row, col, 1, x]
            parts.append(jnp.concatenate([re, im], axis=1))
        rows = jnp.concatenate(parts, axis=0)
        turned = turn(rows)
        flat = jnp.concatenate([rows.reshape(144, 128), turned.reshape(144, 128)], axis=1)
        high, low = split(flat)
        at = row * 6 + x
        boxes_a[at] = flat
        boxes_h[at] = high
        boxes_l[at] = low
        return 0

    lax.fori_loop(0, 6, one, 0)


def lift(line, boxes_h, boxes_l, wide_h, wide_l, cosine, sine, coarse):
    a_high = boxes_h[pl.ds(2 * line, 2)].reshape(288, 256)
    a_low = boxes_l[pl.ds(2 * line, 2)].reshape(288, 256)
    for part in range(4):
        cols = slice(part * 256, (part + 1) * 256)
        value = dot3((a_high, a_low), (wide_h[cols, :], wide_l[cols, :]), NT)
        value = value.reshape(2, 9, 2, 8, 256)
        first = None
        for child in range(4):
            piece = value[child // 2, :, child % 2]
            c = piece * cosine[child : child + 1, cols]
            s = piece * sine[child : child + 1, cols]
            first = c if first is None else first + c
            second = s if child == 0 else second + s
        total = (first + turn(second)).reshape(72, 256)
        for half in range(2):
            coarse[2 * part + half, line] = total[:, half * 128 : (half + 1) * 128]


def move_coarse(coarse, coarse_g, coarse_in):
    def one(mt, _):
        plain = [None] * 9
        turned = [None] * 9
        for sx in range(9):
            for sy in range(9):
                value = None
                for bx in range(3):
                    for by in range(3):
                        row_off, col_off = sx - 3 - bx, sy - 3 - by
                        far = max(abs(row_off), abs(col_off))
                        if far > 3 or far < 2:
                            continue
                        at = OUTER.index((row_off + 3) * 7 + col_off + 3)
                        if value is None:
                            value = coarse[mt, sx, sy * 8 : sy * 8 + 8, :]
                        b = bx * 3 + by
                        row = at * 16 + b
                        p = value * coarse_g[0, mt, row : row + 1, :]
                        q = value * coarse_g[1, mt, row : row + 1, :]
                        plain[b] = p if plain[b] is None else plain[b] + p
                        turned[b] = q if turned[b] is None else turned[b] + q
        for b in range(9):
            coarse_in[mt, b * 8 : b * 8 + 8, :] = plain[b] + turn(turned[b])
        return 0

    lax.fori_loop(0, 8, one, 0)


def lower(coarse_in, wide_h, wide_l, cosine, sine, coarse_y):
    for child in range(4):
        total = None
        for part in range(4):
            cols = slice(part * 256, (part + 1) * 256)
            value = jnp.concatenate(
                [coarse_in[2 * part], coarse_in[2 * part + 1]], axis=1
            ).reshape(9, 8, 256)
            shifted = value * cosine[child : child + 1, cols] - turn(value) * sine[
                child : child + 1, cols
            ]
            y = dot3(split(shifted.reshape(72, 256)), (wide_h[cols, :], wide_l[cols, :]), NN)
            total = y if total is None else total + y
        coarse_y[child] = total


def radiate(boxes_h, boxes_l, rad_h, rad_l, fine):
    def one(step, _):
        at = 3 + 3 * step
        a_high = boxes_h[pl.ds(at, 3), 16:128, :].reshape(336, 256)
        a_low = boxes_l[pl.ds(at, 3), 16:128, :].reshape(336, 256)
        for part in range(2):
            cols = slice(part * 256, (part + 1) * 256)
            value = dot3((a_high, a_low), (rad_h[cols, :], rad_l[cols, :]), NT)
            value = value.reshape(3, 112, 256)
            for half in range(2):
                fine[2 * part + half, pl.ds(3 * step, 3)] = value[
                    :, :, half * 128 : (half + 1) * 128
                ]
        return 0

    lax.fori_loop(0, 4, one, 0)


def move_fine(fine, fine_g, fine_in):
    def one(step, _):
        kt = step // 2
        h = step % 2
        plain = [None] * 18
        turned = [None] * 18
        for sx in range(9):
            for sy in range(12):
                value = None
                for bx in range(3):
                    for by in range(6):
                        row_off, col_off = sx - 3 - bx, sy - 3 - by
                        far = max(abs(row_off), abs(col_off))
                        if far > 3 or far < 2:
                            continue
                        at = OUTER.index((row_off + 3) * 7 + col_off + 3)
                        if value is None:
                            value = fine[kt, 3 * h + sx, (sy + 1) * 8 : (sy + 2) * 8, :]
                        b = bx * 6 + by
                        row = (at * 3 + bx) * 8 + by
                        p = value * fine_g[0, kt, h, row : row + 1, :]
                        q = value * fine_g[1, kt, h, row : row + 1, :]
                        plain[b] = p if plain[b] is None else plain[b] + p
                        turned[b] = q if turned[b] is None else turned[b] + q
        for b in range(18):
            fine_in[kt, h, b * 8 : b * 8 + 8, :] = plain[b] + turn(turned[b])
        return 0

    lax.fori_loop(0, 8, one, 0)


def near(boxes_a, nb_ref, near_g, near_y):
    total = [None] * 36
    for col in range(3):
        rows = boxes_a[5:13, (5 + col) * 8 : (11 + col) * 8, :].reshape(384, 256)
        high, low = split(rows)
        for row in range(3):
            o = row * 3 + col
            block = split(jnp.concatenate([nb_ref[0, o], nb_ref[1, o]], axis=1))
            at = slice(48 * row, 48 * row + 288)
            z = dot3((high[at], low[at]), block, NT)
            for b in range(36):
                mask = near_g[o, b // 6, b % 6 : b % 6 + 1, :]
                term = z[b * 8 : b * 8 + 8] * mask
                if o == 0:
                    near_y[b] = term
                else:
                    near_y[b] += term


def finish(fine_in, rad_h, rad_l, coarse_y, near_y, out_ref):
    scale = 1.0 / math.sqrt(512)
    for h in range(2):
        total = None
        for part in range(2):
            cols = slice(part * 256, (part + 1) * 256)
            value = jnp.concatenate([fine_in[2 * part, h], fine_in[2 * part + 1, h]], axis=1)
            y = dot3(split(value), (rad_h[cols, :], rad_l[cols, :]), NN)
            total = y if total is None else total + y
        for b in range(18):
            x, yy = 3 * h + b // 6, b % 6
            child = 2 * (x % 2) + yy % 2
            parent = (x // 2) * 3 + yy // 2
            far = total[b * 8 : b * 8 + 8] + coarse_y[child, parent * 8 : parent * 8 + 8, :]
            value = (far[:, :128] - turn(far[:, 128:])) * scale + near_y[x * 6 + yy]
            out_ref[0, x, yy] = value[0:4]
            out_ref[1, x, yy] = value[4:8]


SCRATCH = dict(
    tiles=((3, 3, 2, 6, 6, 4, 128), F32),
    rad=((2, 512, 128), F32),
    interp=((1024, 512), F32),
    tf=((49, 2, 512), F32),
    tc=((49, 2, 1024), F32),
    phase=((4, 1024), F32),
    blocks=((2, 9, 128, 128), F32),
    ff=((6, 6, 49), jnp.int32),
    fc=((3, 48, 49), jnp.int32),
    nm=((6, 6, 9), jnp.int32),
    rad_h=((512, 256), BF16),
    rad_l=((512, 256), BF16),
    wide_h=((1024, 256), BF16),
    wide_l=((1024, 256), BF16),
    fine_g=((2, 4, 2, 960, 128), F32),
    coarse_g=((2, 8, 640, 128), F32),
    near_g=((9, 6, 8, 128), F32),
    listed=((16, 128), F32),
    boxes_a=((18, 144, 256), F32),
    boxes_h=((18, 144, 256), BF16),
    boxes_l=((18, 144, 256), BF16),
    cosine=((4, 1024), F32),
    sine=((4, 1024), F32),
    coarse=((8, 9, 72, 128), F32),
    coarse_in=((8, 72, 128), F32),
    coarse_y=((4, 72, 256), F32),
    fine=((4, 12, 112, 128), F32),
    fine_in=((4, 2, 144, 128), F32),
    near_y=((36, 8, 128), F32),
)


LOCAL = ("rad", "interp", "tf", "tc", "phase", "blocks", "ff", "fc", "nm")
MESH = pl.DeviceIdType.MESH


def kernel(
    src_ref, rad_ref, interp_ref, tf_ref, tc_ref, ph_ref, nb_ref, ff_ref, fc_ref, nm_ref, out_ref, *scratch
):
    s = dict(zip(SCRATCH, scratch))
    local_sem, own_sem, send_sem, recv_sem = scratch[len(SCRATCH) :]
    tiles = s["tiles"]
    box = lax.axis_index("box")
    col = lax.axis_index("dir")
    boxes_all = lax.axis_size("box")
    cols_all = lax.axis_size("dir")
    core = col % 2
    outer = col - 1 + 2 * core
    partner = col + 1 - 2 * core
    outer_at = 2 * core
    partner_at = 2 - 2 * core
    above = box < boxes_all - 1
    below = box > 0
    beside = jnp.logical_and(col > 0, col < cols_all - 1)

    own = pltpu.make_async_copy(src_ref, tiles.at[1, 1], own_sem)
    own.start()
    given = (rad_ref, interp_ref, tf_ref, tc_ref, ph_ref, nb_ref, ff_ref, fc_ref, nm_ref)
    loads = {
        name: pltpu.make_async_copy(ref, s[name], local_sem.at[at])
        for at, (name, ref) in enumerate(zip(LOCAL, given))
    }
    for name in ("ff", "fc", "nm", "tc", "tf", "phase", "rad", "interp", "blocks"):
        loads[name].start()

    barrier = pltpu.get_barrier_semaphore()
    for cond, where in (
        (above, (box + 1, col)),
        (below, (box - 1, col)),
        (beside, (box, outer)),
        (None, (box, partner)),
    ):
        if cond is None:
            pl.semaphore_signal(barrier, inc=1, device_id=where, device_id_type=MESH)
        else:

            @pl.when(cond)
            def _(where=where):
                pl.semaphore_signal(barrier, inc=1, device_id=where, device_id_type=MESH)

    peers = 1 + sum(jnp.where(cond, 1, 0) for cond in (above, below, beside))
    pl.semaphore_wait(barrier, peers)

    def copies(at, here, there, where):
        return [
            pltpu.make_async_remote_copy(
                src_ref=tiles.at[here[0], here[1], plane],
                dst_ref=tiles.at[there[0], there[1], plane],
                send_sem=send_sem.at[at, plane],
                recv_sem=recv_sem.at[at, plane],
                device_id=where,
                device_id_type=MESH,
            )
            for plane in range(2)
        ]

    to_outer = copies(0, (1, 1), (1, partner_at), (box, outer))
    to_above = copies(1, (1, 1), (0, 1), (box + 1, col))
    to_below = copies(2, (1, 1), (2, 1), (box - 1, col))
    to_partner = copies(3, (1, 1), (1, outer_at), (box, partner))
    relay_above = copies(4, (1, outer_at), (0, outer_at), (box + 1, col))
    relay_below = copies(5, (1, outer_at), (2, outer_at), (box - 1, col))
    pass_low = copies(6, (0, 1), (0, outer_at), (box, partner))
    pass_high = copies(7, (2, 1), (2, outer_at), (box, partner))
    from_outer = copies(0, (1, 1), (1, outer_at), (box, outer))
    from_below = to_above
    from_above = to_below

    own.wait()

    @pl.when(beside)
    def _():
        for c in to_outer:
            c.start()

    @pl.when(above)
    def _():
        for c in to_above:
            c.start()

    @pl.when(below)
    def _():
        for c in to_below:
            c.start()

    for c in to_partner:
        c.start()

    @pl.when(jnp.logical_not(below))
    def _():
        tiles[0] = jnp.zeros(tiles.shape[1:], F32)

    @pl.when(jnp.logical_not(above))
    def _():
        tiles[2] = jnp.zeros(tiles.shape[1:], F32)

    for edge, at in ((0, 0), (cols_all - 1, 2)):

        @pl.when(col == edge)
        def _(at=at):
            tiles[:, at] = jnp.zeros((3,) + tiles.shape[2:], F32)

    for name in ("ff", "fc", "nm", "tc", "tf"):
        loads[name].wait()
    tables(
        s["tf"], s["tc"], s["ff"], s["fc"], s["nm"], s["fine_g"], s["coarse_g"], s["near_g"], s["listed"],
        col * 3,
    )

    @pl.when(below)
    def _():
        for c in from_below:
            c.wait_recv()
        for c in pass_low:
            c.start()

    @pl.when(above)
    def _():
        for c in from_above:
            c.wait_recv()
        for c in pass_high:
            c.start()

    for name in ("phase", "rad", "interp", "blocks"):
        loads[name].wait()
    s["cosine"][...] = jnp.cos(s["phase"][...])
    s["sine"][...] = jnp.sin(s["phase"][...])
    weights(s["rad"], s["interp"], s["rad_h"], s["rad_l"], s["wide_h"], s["wide_l"])

    for plane in range(2):

        @pl.when(beside)
        def _(plane=plane):
            from_outer[plane].wait_recv()

            @pl.when(above)
            def _():
                relay_above[plane].start()

            @pl.when(below)
            def _():
                relay_below[plane].start()

    for c in to_partner:
        c.wait()

    @pl.when(below)
    def _():
        for c in pass_low:
            c.wait()

    @pl.when(above)
    def _():
        for c in pass_high:
            c.wait()

    @pl.when(jnp.logical_and(beside, below))
    def _():
        for c in relay_above:
            c.wait_recv()

    @pl.when(jnp.logical_and(beside, above))
    def _():
        for c in relay_below:
            c.wait_recv()

    for row in range(3):
        arrange(tiles, row, s["boxes_a"], s["boxes_h"], s["boxes_l"])

    def line(i, _):
        lift(i, s["boxes_h"], s["boxes_l"], s["wide_h"], s["wide_l"], s["cosine"], s["sine"], s["coarse"])
        return 0

    lax.fori_loop(0, 9, line, 0)
    radiate(s["boxes_h"], s["boxes_l"], s["rad_h"], s["rad_l"], s["fine"])
    near(s["boxes_a"], s["blocks"], s["near_g"], s["near_y"])
    move_fine(s["fine"], s["fine_g"], s["fine_in"])
    move_coarse(s["coarse"], s["coarse_g"], s["coarse_in"])
    lower(s["coarse_in"], s["wide_h"], s["wide_l"], s["cosine"], s["sine"], s["coarse_y"])
    finish(s["fine_in"], s["rad_h"], s["rad_l"], s["coarse_y"], s["near_y"], out_ref)

    for cond, sent in ((beside, to_outer), (above, to_above), (below, to_below)):

        @pl.when(cond)
        def _(sent=sent):
            for c in sent:
                c.wait_send()

    for cond, sent in ((above, relay_above), (below, relay_below)):

        @pl.when(jnp.logical_and(beside, cond))
        def _(sent=sent):
            for c in sent:
                c.wait_send()


def body(
    sources, radiation, interp, trans_fine, trans_coarse, child_phase, near_block, far_fine, far_coarse, near_mask
):
    anywhere = pl.BlockSpec(memory_space=pl.ANY)
    out = pl.pallas_call(
        kernel,
        out_shape=jax.ShapeDtypeStruct((2, 6, 6, 4, 128), F32),
        in_specs=[anywhere] * 10,
        out_specs=pl.BlockSpec(memory_space=pltpu.VMEM),
        scratch_shapes=[pltpu.VMEM(*v) for v in SCRATCH.values()]
        + [
            pltpu.SemaphoreType.DMA((len(LOCAL),)),
            pltpu.SemaphoreType.DMA,
            pltpu.SemaphoreType.DMA((8, 2)),
            pltpu.SemaphoreType.DMA((8, 2)),
        ],
        compiler_params=pltpu.CompilerParams(
            vmem_limit_bytes=60 << 20, collective_id=0, has_side_effects=True
        ),
        name="product",
    )(
        jnp.transpose(sources, (0, 2, 3, 1, 4)),
        radiation,
        interp,
        jnp.transpose(trans_fine, (1, 0, 2)),
        jnp.transpose(trans_coarse, (1, 0, 2)),
        child_phase,
        near_block,
        far_fine,
        far_coarse,
        near_mask,
    )
    return jnp.transpose(out, (0, 3, 1, 2, 4))


def solution(mesh):
    placed = (
        P(None, None, "box", "dir", None),
        P(),
        P(),
        P(),
        P(),
        P(),
        P(),
        P("box", "dir", None),
        P("box", None, None),
        P("box", "dir", None),
    )
    return jax.shard_map(
        body,
        mesh=mesh,
        in_specs=placed,
        out_specs=P(None, None, "box", "dir", None),
        check_vma=False,
    )
```

profile of v0, /device:TPU:30, one launch (start us, length us, event | category | flops | bytes accessed | tf_op | source)
XLA Modules:
  0.0 40.5 jit_solution(14592712109099357659)
XLA Ops:
  0.0 38.9 %product.1 = f32[2,6,6,4,128]{4,3,2,1,0:T(4,128)} custom-call(f32[2,6,6,4,128]{4,3,2,1,0:T(4,128)} %bitcast.7, f32[2,512,128]{2,1,0:T(8,128)} %rad_ref.1, f32[1024,512]{1,0:T(8,128)} %interp_ref.1, f32[49,2,512]{2,1,0:T(2,128)} %bitcast.6, f32[49,2,1024]{2,1,0:T(2,128)} %bitcast.5, f32[4,1024]{1,0:T(4,128)} %ph_ref.1, f32[2,9,128,128]{3,2,1,0:T(8,128)} %nb_ref.1, ...), custom_call_target="tpu_custom_call" | custom-call | tf_op jit(solution)/shard_map/product/pallas_call | solution.py:496
  39.0 1.6 %copy.12 = f32[2,4,6,6,128]{4,1,3,2,0:T(4,128)} copy(f32[2,4,6,6,128]{4,1,3,2,0:T(4,128)} %bitcast.4) | data formatting | bytes 294912
where the time goes:
time: 40.6 us; the launch traced here: 40.5 us
  Pallas kernels  38.9 us (96%)
  local copies, waits for them, and re-layouts  1.58 us (4%)
    pallas_call x1, Pallas kernels, body(): pl.pallas_call(kernel, out_shape=jax.ShapeDtypeStruct((2, 6, 6, 4, 128),...  38.9 us
    unnamed x1, local copies, waits for them, and re-layouts  1.58 us

commit v1 on v0

--- a/solution.py
+++ b/solution.py
@@ -81,51 +81,51 @@
             near_g[o, x, 0:6, :] = jnp.broadcast_to(near[:, o : o + 1], (6, 128))
 
 
-def arrange(tiles, row, boxes_a, boxes_h, boxes_l):
+def arrange(tiles, row, col, boxes_a, boxes_h, boxes_l):
     def one(x, _):
-        parts = []
-        for col in range(3):
-            re = tiles[row, col, 0, x]
-            im = tiles[row, col, 1, x]
-            parts.append(jnp.concatenate([re, im], axis=1))
-        rows = jnp.concatenate(parts, axis=0)
-        turned = turn(rows)
-        flat = jnp.concatenate([rows.reshape(144, 128), turned.reshape(144, 128)], axis=1)
+        rows = jnp.concatenate([tiles[row, col, 0, x], tiles[row, col, 1, x]], axis=1)
+        flat = jnp.concatenate([rows.reshape(48, 128), turn(rows).reshape(48, 128)], axis=1)
         high, low = split(flat)
         at = row * 6 + x
-        boxes_a[at] = flat
-        boxes_h[at] = high
-        boxes_l[at] = low
+        where = pl.ds(pl.multiple_of(col * 48, 16), 48)
+        boxes_a[at, where, :] = flat
+        boxes_h[at, where, :] = high
+        boxes_l[at, where, :] = low
         return 0
 
     lax.fori_loop(0, 6, one, 0)
 
 
-def lift(line, boxes_h, boxes_l, wide_h, wide_l, cosine, sine, coarse):
-    a_high = boxes_h[pl.ds(2 * line, 2)].reshape(288, 256)
-    a_low = boxes_l[pl.ds(2 * line, 2)].reshape(288, 256)
+def lift(line, lines, col, cols_here, boxes_h, boxes_l, wide_h, wide_l, cosine, sine, coarse):
+    at = pl.ds(pl.multiple_of(col * 48, 16), 48 * cols_here)
+    count = 96 * lines * cols_here
+    a_high = boxes_h[pl.ds(2 * line, 2 * lines), at, :].reshape(count, 256)
+    a_low = boxes_l[pl.ds(2 * line, 2 * lines), at, :].reshape(count, 256)
     for part in range(4):
         cols = slice(part * 256, (part + 1) * 256)
         value = dot3((a_high, a_low), (wide_h[cols, :], wide_l[cols, :]), NT)
-        value = value.reshape(2, 9, 2, 8, 256)
+        value = value.reshape(lines, 2, 3 * cols_here, 2, 8, 256)
         first = None
         for child in range(4):
-            piece = value[child // 2, :, child % 2]
+            piece = value[:, child // 2, :, child % 2]
             c = piece * cosine[child : child + 1, cols]
             s = piece * sine[child : child + 1, cols]
             first = c if first is None else first + c
             second = s if child == 0 else second + s
-        total = (first + turn(second)).reshape(72, 256)
+        total = (first + turn(second)).reshape(lines, 24 * cols_here, 256)
+        where = pl.ds(pl.multiple_of(col * 24, 8), 24 * cols_here)
         for half in range(2):
-            coarse[2 * part + half, line] = total[:, half * 128 : (half + 1) * 128]
-
-
-def move_coarse(coarse, coarse_g, coarse_in):
+            coarse[2 * part + half, pl.ds(line, lines), where, :] = total[
+                :, :, half * 128 : (half + 1) * 128
+            ]
+
+
+def move_coarse(coarse, coarse_g, coarse_in, columns, add):
     def one(mt, _):
         plain = [None] * 9
         turned = [None] * 9
         for sx in range(9):
-            for sy in range(9):
+            for sy in columns:
                 value = None
                 for bx in range(3):
                     for by in range(3):
@@ -143,7 +143,12 @@
                         plain[b] = p if plain[b] is None else plain[b] + p
                         turned[b] = q if turned[b] is None else turned[b] + q
         for b in range(9):
-            coarse_in[mt, b * 8 : b * 8 + 8, :] = plain[b] + turn(turned[b])
+            if plain[b] is None:
+                continue
+            total = plain[b] + turn(turned[b])
+            if add:
+                total = total + coarse_in[mt, b * 8 : b * 8 + 8, :]
+            coarse_in[mt, b * 8 : b * 8 + 8, :] = total
         return 0
 
     lax.fori_loop(0, 8, one, 0)
@@ -165,32 +170,35 @@
         coarse_y[child] = total
 
 
-def radiate(boxes_h, boxes_l, rad_h, rad_l, fine):
+def radiate(first, count, per, start, rows, boxes_h, boxes_l, rad_h, rad_l, fine):
+    where = pl.ds(pl.multiple_of(start, 16), rows)
+    put = pl.ds(pl.multiple_of(start - 16, 8), rows)
+
     def one(step, _):
-        at = 3 + 3 * step
-        a_high = boxes_h[pl.ds(at, 3), 16:128, :].reshape(336, 256)
-        a_low = boxes_l[pl.ds(at, 3), 16:128, :].reshape(336, 256)
+        at = first + per * step
+        a_high = boxes_h[pl.ds(at, per), where, :].reshape(per * rows, 256)
+        a_low = boxes_l[pl.ds(at, per), where, :].reshape(per * rows, 256)
         for part in range(2):
             cols = slice(part * 256, (part + 1) * 256)
             value = dot3((a_high, a_low), (rad_h[cols, :], rad_l[cols, :]), NT)
-            value = value.reshape(3, 112, 256)
+            value = value.reshape(per, rows, 256)
             for half in range(2):
-                fine[2 * part + half, pl.ds(3 * step, 3)] = value[
+                fine[2 * part + half, pl.ds(at - 3, per), put, :] = value[
                     :, :, half * 128 : (half + 1) * 128
                 ]
         return 0
 
-    lax.fori_loop(0, 4, one, 0)
-
-
-def move_fine(fine, fine_g, fine_in):
+    lax.fori_loop(0, count // per, one, 0)
+
+
+def move_fine(fine, fine_g, fine_in, columns, add):
     def one(step, _):
         kt = step // 2
         h = step % 2
         plain = [None] * 18
         turned = [None] * 18
         for sx in range(9):
-            for sy in range(12):
+            for sy in columns:
                 value = None
                 for bx in range(3):
                     for by in range(6):
@@ -208,29 +216,31 @@
                         plain[b] = p if plain[b] is None else plain[b] + p
                         turned[b] = q if turned[b] is None else turned[b] + q
         for b in range(18):
-            fine_in[kt, h, b * 8 : b * 8 + 8, :] = plain[b] + turn(turned[b])
+            if plain[b] is None:
+                continue
+            total = plain[b] + turn(turned[b])
+            if add:
+                total = total + fine_in[kt, h, b * 8 : b * 8 + 8, :]
+            fine_in[kt, h, b * 8 : b * 8 + 8, :] = total
         return 0
 
     lax.fori_loop(0, 8, one, 0)
 
 
-def near(boxes_a, nb_ref, near_g, near_y):
-    total = [None] * 36
-    for col in range(3):
-        rows = boxes_a[5:13, (5 + col) * 8 : (11 + col) * 8, :].reshape(384, 256)
-        high, low = split(rows)
-        for row in range(3):
-            o = row * 3 + col
-            block = split(jnp.concatenate([nb_ref[0, o], nb_ref[1, o]], axis=1))
-            at = slice(48 * row, 48 * row + 288)
-            z = dot3((high[at], low[at]), block, NT)
-            for b in range(36):
-                mask = near_g[o, b // 6, b % 6 : b % 6 + 1, :]
-                term = z[b * 8 : b * 8 + 8] * mask
-                if o == 0:
-                    near_y[b] = term
-                else:
-                    near_y[b] += term
+def near(col, add, boxes_a, nb_ref, near_g, near_y):
+    rows = boxes_a[5:13, pl.ds(pl.multiple_of((5 + col) * 8, 8), 48), :].reshape(384, 256)
+    high, low = split(rows)
+    for row in range(3):
+        o = row * 3 + col
+        block = split(jnp.concatenate([nb_ref[0, o], nb_ref[1, o]], axis=1))
+        at = slice(48 * row, 48 * row + 288)
+        z = dot3((high[at], low[at]), block, NT)
+        for b in range(36):
+            term = z[b * 8 : b * 8 + 8] * near_g[o, b // 6, b % 6 : b % 6 + 1, :]
+            if row == 0 and not add:
+                near_y[b] = term
+            else:
+                near_y[b] += term
 
 
 def finish(fine_in, rad_h, rad_l, coarse_y, near_y, out_ref):
@@ -402,6 +412,11 @@
         col * 3,
     )
 
+    for name in ("phase", "rad", "interp", "blocks"):
+        loads[name].wait()
+    s["cosine"][...] = jnp.cos(s["phase"][...])
+    s["sine"][...] = jnp.sin(s["phase"][...])
+
     @pl.when(below)
     def _():
         for c in from_below:
@@ -416,12 +431,33 @@
         for c in pass_high:
             c.start()
 
-    for name in ("phase", "rad", "interp", "blocks"):
-        loads[name].wait()
-    s["cosine"][...] = jnp.cos(s["phase"][...])
-    s["sine"][...] = jnp.sin(s["phase"][...])
     weights(s["rad"], s["interp"], s["rad_h"], s["rad_l"], s["wide_h"], s["wide_l"])
-
+    for c in to_partner:
+        c.wait()
+
+    @pl.when(below)
+    def _():
+        for c in pass_low:
+            c.wait()
+
+    @pl.when(above)
+    def _():
+        for c in pass_high:
+            c.wait()
+
+    boxes = (s["boxes_a"], s["boxes_h"], s["boxes_l"])
+    lifted = (s["boxes_h"], s["boxes_l"], s["wide_h"], s["wide_l"], s["cosine"], s["sine"], s["coarse"])
+    sent_out = (s["boxes_h"], s["boxes_l"], s["rad_h"], s["rad_l"], s["fine"])
+    close = (s["boxes_a"], s["blocks"], s["near_g"], s["near_y"])
+    for row in range(3):
+        arrange(tiles, row, 1, *boxes)
+        arrange(tiles, row, partner_at, *boxes)
+
+    def line(i, _):
+        lift(i, 1, 1 - core, 2, *lifted)
+        return 0
+
+    lax.fori_loop(0, 9, line, 0)
     for plane in range(2):
 
         @pl.when(beside)
@@ -436,18 +472,20 @@
             def _():
                 relay_below[plane].start()
 
-    for c in to_partner:
-        c.wait()
-
-    @pl.when(below)
-    def _():
-        for c in pass_low:
-            c.wait()
-
-    @pl.when(above)
-    def _():
-        for c in pass_high:
-            c.wait()
+    radiate(3, 12, 3, 48 - 32 * core, 80, *sent_out)
+    near(1, False, *close)
+    near(partner_at, True, *close)
+    for side in range(2):
+
+        @pl.when(core == side)
+        def _(side=side):
+            inner = range(9) if side else range(3, 12)
+            move_fine(s["fine"], s["fine_g"], s["fine_in"], inner, False)
+            inner = range(6) if side else range(3, 9)
+            move_coarse(s["coarse"], s["coarse_g"], s["coarse_in"], inner, False)
+
+    arrange(tiles, 1, outer_at, *boxes)
+    lift(3, 3, outer_at, 1, *lifted)
 
     @pl.when(jnp.logical_and(beside, below))
     def _():
@@ -459,18 +497,25 @@
         for c in relay_below:
             c.wait_recv()
 
-    for row in range(3):
-        arrange(tiles, row, s["boxes_a"], s["boxes_h"], s["boxes_l"])
-
-    def line(i, _):
-        lift(i, s["boxes_h"], s["boxes_l"], s["wide_h"], s["wide_l"], s["cosine"], s["sine"], s["coarse"])
-        return 0
-
-    lax.fori_loop(0, 9, line, 0)
-    radiate(s["boxes_h"], s["boxes_l"], s["rad_h"], s["rad_l"], s["fine"])
-    near(s["boxes_a"], s["blocks"], s["near_g"], s["near_y"])
-    move_fine(s["fine"], s["fine_g"], s["fine_in"])
-    move_coarse(s["coarse"], s["coarse_g"], s["coarse_in"])
+    arrange(tiles, 0, outer_at, *boxes)
+    arrange(tiles, 2, outer_at, *boxes)
+
+    def rest(i, _):
+        lift(6 * i, 3, outer_at, 1, *lifted)
+        return 0
+
+    lax.fori_loop(0, 2, rest, 0)
+    radiate(3, 12, 6, 16 + 80 * core, 32, *sent_out)
+    near(outer_at, True, *close)
+    for side in range(2):
+
+        @pl.when(core == side)
+        def _(side=side):
+            outside = range(9, 12) if side else range(3)
+            move_fine(s["fine"], s["fine_g"], s["fine_in"], outside, True)
+            outside = range(6, 9) if side else range(3)
+            move_coarse(s["coarse"], s["coarse_g"], s["coarse_in"], outside, True)
+
     lower(s["coarse_in"], s["wide_h"], s["wide_l"], s["cosine"], s["sine"], s["coarse_y"])
     finish(s["fine_in"], s["rad_h"], s["rad_l"], s["coarse_y"], s["near_y"], out_ref)
 

time: 40.6 us -> 38.7 us (0.953)
  the two profiles are of different devices: /device:TPU:30 before, /device:TPU:11 now
where the time goes in v1:
time: 38.7 us; the launch traced here: 38.6 us
  Pallas kernels  37 us (96%)
  local copies, waits for them, and re-layouts  1.58 us (4%)
    pallas_call x1, Pallas kernels, body(): pl.pallas_call(kernel, out_shape=jax.ShapeDtypeStruct((2, 6, 6, 4, 128),...  37 us
    unnamed x1, local copies, waits for them, and re-layouts  1.58 us

profile of v1, /device:TPU:11, one launch (start us, length us, event | category | flops | bytes accessed | tf_op | source)
XLA Modules:
  0.0 38.6 jit_solution(6261146767908144473)
XLA Ops:
  0.0 37.0 %product.1 = f32[2,6,6,4,128]{4,3,2,1,0:T(4,128)} custom-call(f32[2,6,6,4,128]{4,3,2,1,0:T(4,128)} %bitcast.7, f32[2,512,128]{2,1,0:T(8,128)} %rad_ref.1, f32[1024,512]{1,0:T(8,128)} %interp_ref.1, f32[49,2,512]{2,1,0:T(2,128)} %bitcast.6, f32[49,2,1024]{2,1,0:T(2,128)} %bitcast.5, f32[4,1024]{1,0:T(4,128)} %ph_ref.1, f32[2,9,128,128]{3,2,1,0:T(8,128)} %nb_ref.1, ...), custom_call_target="tpu_custom_call" | custom-call | tf_op jit(solution)/shard_map/product/pallas_call | solution.py:541
  37.1 1.6 %copy.12 = f32[2,4,6,6,128]{4,1,3,2,0:T(4,128)} copy(f32[2,4,6,6,128]{4,1,3,2,0:T(4,128)} %bitcast.4) | data formatting | bytes 294912

commit v2 on v1

--- a/solution.py
+++ b/solution.py
@@ -42,14 +42,14 @@
         rad_l[:, plane * 128 : (plane + 1) * 128] = low
 
     def some(step, _):
-        rows = pl.ds(pl.multiple_of(step * 256, 256), 256)
+        rows = pl.ds(pl.multiple_of(step * 512, 512), 512)
         value = dot3(split(interp_ref[rows, :]), (rad_h[...], rad_l[...]), NN)
         high, low = split(value)
         wide_h[rows, :] = high
         wide_l[rows, :] = low
         return 0
 
-    lax.fori_loop(0, 4, some, 0)
+    lax.fori_loop(0, 2, some, 0)
 
 
 def tables(tf_ref, tc_ref, ff_ref, fc_ref, nm_ref, fine_g, coarse_g, near_g, listed, first):
@@ -120,12 +120,12 @@
             ]
 
 
-def move_coarse(coarse, coarse_g, coarse_in, columns, add):
+def move_coarse(coarse, coarse_g, coarse_in):
     def one(mt, _):
         plain = [None] * 9
         turned = [None] * 9
         for sx in range(9):
-            for sy in columns:
+            for sy in range(9):
                 value = None
                 for bx in range(3):
                     for by in range(3):
@@ -143,31 +143,29 @@
                         plain[b] = p if plain[b] is None else plain[b] + p
                         turned[b] = q if turned[b] is None else turned[b] + q
         for b in range(9):
-            if plain[b] is None:
-                continue
-            total = plain[b] + turn(turned[b])
-            if add:
-                total = total + coarse_in[mt, b * 8 : b * 8 + 8, :]
-            coarse_in[mt, b * 8 : b * 8 + 8, :] = total
+            coarse_in[mt, b * 8 : b * 8 + 8, :] = plain[b] + turn(turned[b])
         return 0
 
     lax.fori_loop(0, 8, one, 0)
 
 
 def lower(coarse_in, wide_h, wide_l, cosine, sine, coarse_y):
-    for child in range(4):
-        total = None
-        for part in range(4):
-            cols = slice(part * 256, (part + 1) * 256)
-            value = jnp.concatenate(
-                [coarse_in[2 * part], coarse_in[2 * part + 1]], axis=1
-            ).reshape(9, 8, 256)
-            shifted = value * cosine[child : child + 1, cols] - turn(value) * sine[
-                child : child + 1, cols
-            ]
-            y = dot3(split(shifted.reshape(72, 256)), (wide_h[cols, :], wide_l[cols, :]), NN)
-            total = y if total is None else total + y
-        coarse_y[child] = total
+    total = None
+    for part in range(4):
+        cols = slice(part * 256, (part + 1) * 256)
+        value = jnp.concatenate(
+            [coarse_in[2 * part], coarse_in[2 * part + 1]], axis=1
+        ).reshape(9, 8, 256)
+        other = turn(value)
+        shifted = [
+            (value * cosine[child : child + 1, cols] - other * sine[child : child + 1, cols]).reshape(72, 256)
+            for child in range(4)
+        ]
+        y = dot3(
+            split(jnp.concatenate(shifted, axis=0)), (wide_h[cols, :], wide_l[cols, :]), NN
+        )
+        total = y if total is None else total + y
+    coarse_y[...] = total.reshape(4, 72, 256)
 
 
 def radiate(first, count, per, start, rows, boxes_h, boxes_l, rad_h, rad_l, fine):
@@ -245,21 +243,22 @@
 
 def finish(fine_in, rad_h, rad_l, coarse_y, near_y, out_ref):
     scale = 1.0 / math.sqrt(512)
-    for h in range(2):
-        total = None
-        for part in range(2):
-            cols = slice(part * 256, (part + 1) * 256)
-            value = jnp.concatenate([fine_in[2 * part, h], fine_in[2 * part + 1, h]], axis=1)
-            y = dot3(split(value), (rad_h[cols, :], rad_l[cols, :]), NN)
-            total = y if total is None else total + y
-        for b in range(18):
-            x, yy = 3 * h + b // 6, b % 6
-            child = 2 * (x % 2) + yy % 2
-            parent = (x // 2) * 3 + yy // 2
-            far = total[b * 8 : b * 8 + 8] + coarse_y[child, parent * 8 : parent * 8 + 8, :]
-            value = (far[:, :128] - turn(far[:, 128:])) * scale + near_y[x * 6 + yy]
-            out_ref[0, x, yy] = value[0:4]
-            out_ref[1, x, yy] = value[4:8]
+    total = None
+    for part in range(2):
+        cols = slice(part * 256, (part + 1) * 256)
+        value = jnp.concatenate(
+            [fine_in[2 * part].reshape(288, 128), fine_in[2 * part + 1].reshape(288, 128)], axis=1
+        )
+        y = dot3(split(value), (rad_h[cols, :], rad_l[cols, :]), NN)
+        total = y if total is None else total + y
+    for b in range(36):
+        x, yy = b // 6, b % 6
+        child = 2 * (x % 2) + yy % 2
+        parent = (x // 2) * 3 + yy // 2
+        far = total[b * 8 : b * 8 + 8] + coarse_y[child, parent * 8 : parent * 8 + 8, :]
+        value = (far[:, :128] - turn(far[:, 128:])) * scale + near_y[b]
+        out_ref[0, x, yy] = value[0:4]
+        out_ref[1, x, yy] = value[4:8]
 
 
 SCRATCH = dict(
@@ -303,7 +302,7 @@
     src_ref, rad_ref, interp_ref, tf_ref, tc_ref, ph_ref, nb_ref, ff_ref, fc_ref, nm_ref, out_ref, *scratch
 ):
     s = dict(zip(SCRATCH, scratch))
-    local_sem, own_sem, send_sem, recv_sem = scratch[len(SCRATCH) :]
+    local_sem, own_sem, send_sem, recv_sem, share_sem = scratch[len(SCRATCH) :]
     tiles = s["tiles"]
     box = lax.axis_index("box")
     col = lax.axis_index("dir")
@@ -373,7 +372,10 @@
 
     own.wait()
 
-    @pl.when(beside)
+    lines_z = boxes_all // 2
+    late = jnp.logical_or(box % lines_z == 0, box % lines_z == lines_z - 1)
+
+    @pl.when(jnp.logical_and(beside, jnp.logical_not(late)))
     def _():
         for c in to_outer:
             c.start()
@@ -412,11 +414,24 @@
         col * 3,
     )
 
+    @pl.when(jnp.logical_and(beside, late))
+    def _():
+        for c in to_outer:
+            c.start()
+
     for name in ("phase", "rad", "interp", "blocks"):
         loads[name].wait()
     s["cosine"][...] = jnp.cos(s["phase"][...])
     s["sine"][...] = jnp.sin(s["phase"][...])
 
+    weights(s["rad"], s["interp"], s["rad_h"], s["rad_l"], s["wide_h"], s["wide_l"])
+    boxes = (s["boxes_a"], s["boxes_h"], s["boxes_l"])
+    lifted = (s["boxes_h"], s["boxes_l"], s["wide_h"], s["wide_l"], s["cosine"], s["sine"], s["coarse"])
+    sent_out = (s["boxes_h"], s["boxes_l"], s["rad_h"], s["rad_l"], s["fine"])
+    close = (s["boxes_a"], s["blocks"], s["near_g"], s["near_y"])
+    arrange(tiles, 1, 1, *boxes)
+    lift(3, 3, 1, 1, *lifted)
+
     @pl.when(below)
     def _():
         for c in from_below:
@@ -431,33 +446,14 @@
         for c in pass_high:
             c.start()
 
-    weights(s["rad"], s["interp"], s["rad_h"], s["rad_l"], s["wide_h"], s["wide_l"])
-    for c in to_partner:
-        c.wait()
-
-    @pl.when(below)
-    def _():
-        for c in pass_low:
-            c.wait()
-
-    @pl.when(above)
-    def _():
-        for c in pass_high:
-            c.wait()
-
-    boxes = (s["boxes_a"], s["boxes_h"], s["boxes_l"])
-    lifted = (s["boxes_h"], s["boxes_l"], s["wide_h"], s["wide_l"], s["cosine"], s["sine"], s["coarse"])
-    sent_out = (s["boxes_h"], s["boxes_l"], s["rad_h"], s["rad_l"], s["fine"])
-    close = (s["boxes_a"], s["blocks"], s["near_g"], s["near_y"])
-    for row in range(3):
-        arrange(tiles, row, 1, *boxes)
-        arrange(tiles, row, partner_at, *boxes)
-
-    def line(i, _):
-        lift(i, 1, 1 - core, 2, *lifted)
+    arrange(tiles, 0, 1, *boxes)
+    arrange(tiles, 2, 1, *boxes)
+
+    def ends(i, _):
+        lift(6 * i, 3, 1, 1, *lifted)
         return 0
 
-    lax.fori_loop(0, 9, line, 0)
+    lax.fori_loop(0, 2, ends, 0)
     for plane in range(2):
 
         @pl.when(beside)
@@ -472,7 +468,33 @@
             def _():
                 relay_below[plane].start()
 
-    radiate(3, 12, 3, 48 - 32 * core, 80, *sent_out)
+    for c in to_partner:
+        c.wait()
+    arrange(tiles, 1, partner_at, *boxes)
+
+    share = pltpu.make_async_remote_copy(
+        src_ref=s["coarse"].at[:, :, 24:48, :],
+        dst_ref=s["coarse"].at[:, :, pl.ds(pl.multiple_of(24 * outer_at, 8), 24), :],
+        send_sem=share_sem.at[0],
+        recv_sem=share_sem.at[1],
+        device_id=(box, partner),
+        device_id_type=MESH,
+    )
+    share.start()
+
+    @pl.when(below)
+    def _():
+        for c in pass_low:
+            c.wait()
+
+    @pl.when(above)
+    def _():
+        for c in pass_high:
+            c.wait()
+
+    arrange(tiles, 0, partner_at, *boxes)
+    arrange(tiles, 2, partner_at, *boxes)
+    radiate(3, 12, 6, 48 - 32 * core, 80, *sent_out)
     near(1, False, *close)
     near(partner_at, True, *close)
     for side in range(2):
@@ -481,11 +503,8 @@
         def _(side=side):
             inner = range(9) if side else range(3, 12)
             move_fine(s["fine"], s["fine_g"], s["fine_in"], inner, False)
-            inner = range(6) if side else range(3, 9)
-            move_coarse(s["coarse"], s["coarse_g"], s["coarse_in"], inner, False)
 
     arrange(tiles, 1, outer_at, *boxes)
-    lift(3, 3, outer_at, 1, *lifted)
 
     @pl.when(jnp.logical_and(beside, below))
     def _():
@@ -499,13 +518,8 @@
 
     arrange(tiles, 0, outer_at, *boxes)
     arrange(tiles, 2, outer_at, *boxes)
-
-    def rest(i, _):
-        lift(6 * i, 3, outer_at, 1, *lifted)
-        return 0
-
-    lax.fori_loop(0, 2, rest, 0)
-    radiate(3, 12, 6, 16 + 80 * core, 32, *sent_out)
+    lift(0, 9, outer_at, 1, *lifted)
+    radiate(3, 12, 12, 16 + 80 * core, 32, *sent_out)
     near(outer_at, True, *close)
     for side in range(2):
 
@@ -513,9 +527,9 @@
         def _(side=side):
             outside = range(9, 12) if side else range(3)
             move_fine(s["fine"], s["fine_g"], s["fine_in"], outside, True)
-            outside = range(6, 9) if side else range(3)
-            move_coarse(s["coarse"], s["coarse_g"], s["coarse_in"], outside, True)
-
+
+    share.wait()
+    move_coarse(s["coarse"], s["coarse_g"], s["coarse_in"])
     lower(s["coarse_in"], s["wide_h"], s["wide_l"], s["cosine"], s["sine"], s["coarse_y"])
     finish(s["fine_in"], s["rad_h"], s["rad_l"], s["coarse_y"], s["near_y"], out_ref)
 
@@ -549,6 +563,7 @@
             pltpu.SemaphoreType.DMA,
             pltpu.SemaphoreType.DMA((8, 2)),
             pltpu.SemaphoreType.DMA((8, 2)),
+            pltpu.SemaphoreType.DMA((2,)),
         ],
         compiler_params=pltpu.CompilerParams(
             vmem_limit_bytes=60 << 20, collective_id=0, has_side_effects=True

time: 38.7 us -> 30.5 us (0.79)
  Pallas kernels: 37 us -> 28.8 us
    pallas_call x1, Pallas kernels: 37 us -> 28.8 us  [body(): pl.pallas_call(kernel, out_shape=jax.ShapeDtypeStruct((2, 6, 6, 4, 128),...]
where the time goes in v2:
time: 30.5 us; the launch traced here: 30.4 us
  Pallas kernels  28.8 us (94%)
  local copies, waits for them, and re-layouts  1.58 us (5%)
    pallas_call x1, Pallas kernels, body(): pl.pallas_call(kernel, out_shape=jax.ShapeDtypeStruct((2, 6, 6, 4, 128),...  28.8 us
    unnamed x1, local copies, waits for them, and re-layouts  1.58 us

profile of v2, /device:TPU:11, one launch (start us, length us, event | category | flops | bytes accessed | tf_op | source)
XLA Modules:
  0.0 30.4 jit_solution(8384281221363046812)
XLA Ops:
  0.0 28.8 %product.1 = f32[2,6,6,4,128]{4,3,2,1,0:T(4,128)} custom-call(f32[2,6,6,4,128]{4,3,2,1,0:T(4,128)} %bitcast.7, f32[2,512,128]{2,1,0:T(8,128)} %rad_ref.1, f32[1024,512]{1,0:T(8,128)} %interp_ref.1, f32[49,2,512]{2,1,0:T(2,128)} %bitcast.6, f32[49,2,1024]{2,1,0:T(2,128)} %bitcast.5, f32[4,1024]{1,0:T(4,128)} %ph_ref.1, f32[2,9,128,128]{3,2,1,0:T(8,128)} %nb_ref.1, ...), custom_call_target="tpu_custom_call" | custom-call | tf_op jit(solution)/shard_map/product/pallas_call | solution.py:555
  28.8 1.6 %copy.12 = f32[2,4,6,6,128]{4,1,3,2,0:T(4,128)} copy(f32[2,4,6,6,128]{4,1,3,2,0:T(4,128)} %bitcast.4) | data formatting | bytes 294912

commit v3 on v2

--- a/solution.py
+++ b/solution.py
@@ -168,12 +168,12 @@
     coarse_y[...] = total.reshape(4, 72, 256)
 
 
-def radiate(first, count, per, start, rows, boxes_h, boxes_l, rad_h, rad_l, fine):
+def radiate(first, stride, steps, per, start, rows, boxes_h, boxes_l, rad_h, rad_l, fine):
     where = pl.ds(pl.multiple_of(start, 16), rows)
     put = pl.ds(pl.multiple_of(start - 16, 8), rows)
 
     def one(step, _):
-        at = first + per * step
+        at = first + stride * step
         a_high = boxes_h[pl.ds(at, per), where, :].reshape(per * rows, 256)
         a_low = boxes_l[pl.ds(at, per), where, :].reshape(per * rows, 256)
         for part in range(2):
@@ -186,43 +186,42 @@
                 ]
         return 0
 
-    lax.fori_loop(0, count // per, one, 0)
-
-
-def move_fine(fine, fine_g, fine_in, columns, add):
-    def one(step, _):
-        kt = step // 2
-        h = step % 2
-        plain = [None] * 18
-        turned = [None] * 18
-        for sx in range(9):
-            for sy in columns:
-                value = None
-                for bx in range(3):
-                    for by in range(6):
-                        row_off, col_off = sx - 3 - bx, sy - 3 - by
-                        far = max(abs(row_off), abs(col_off))
-                        if far > 3 or far < 2:
-                            continue
-                        at = OUTER.index((row_off + 3) * 7 + col_off + 3)
-                        if value is None:
-                            value = fine[kt, 3 * h + sx, (sy + 1) * 8 : (sy + 2) * 8, :]
-                        b = bx * 6 + by
-                        row = (at * 3 + bx) * 8 + by
-                        p = value * fine_g[0, kt, h, row : row + 1, :]
-                        q = value * fine_g[1, kt, h, row : row + 1, :]
-                        plain[b] = p if plain[b] is None else plain[b] + p
-                        turned[b] = q if turned[b] is None else turned[b] + q
-        for b in range(18):
-            if plain[b] is None:
-                continue
-            total = plain[b] + turn(turned[b])
-            if add:
-                total = total + fine_in[kt, h, b * 8 : b * 8 + 8, :]
-            fine_in[kt, h, b * 8 : b * 8 + 8, :] = total
+    lax.fori_loop(0, steps, one, 0)
+
+
+def move_fine(fine, fine_g, fine_in, lines, columns, add):
+    def one(kt, _):
+        for h in range(2):
+            plain = [None] * 18
+            turned = [None] * 18
+            for x in lines:
+                for sy in columns:
+                    value = None
+                    for bx in range(3):
+                        for by in range(6):
+                            row_off, col_off = x - 3 * h - 3 - bx, sy - 3 - by
+                            far = max(abs(row_off), abs(col_off))
+                            if far > 3 or far < 2:
+                                continue
+                            at = OUTER.index((row_off + 3) * 7 + col_off + 3)
+                            if value is None:
+                                value = fine[kt, x, (sy + 1) * 8 : (sy + 2) * 8, :]
+                            b = bx * 6 + by
+                            row = (at * 3 + bx) * 8 + by
+                            p = value * fine_g[0, kt, h, row : row + 1, :]
+                            q = value * fine_g[1, kt, h, row : row + 1, :]
+                            plain[b] = p if plain[b] is None else plain[b] + p
+                            turned[b] = q if turned[b] is None else turned[b] + q
+            for b in range(18):
+                if plain[b] is None:
+                    continue
+                total = plain[b] + turn(turned[b])
+                if add:
+                    total = total + fine_in[kt, h, b * 8 : b * 8 + 8, :]
+                fine_in[kt, h, b * 8 : b * 8 + 8, :] = total
         return 0
 
-    lax.fori_loop(0, 8, one, 0)
+    lax.fori_loop(0, 4, one, 0)
 
 
 def near(col, add, boxes_a, nb_ref, near_g, near_y):
@@ -432,6 +431,31 @@
     arrange(tiles, 1, 1, *boxes)
     lift(3, 3, 1, 1, *lifted)
 
+    for c in to_partner:
+        c.wait()
+    arrange(tiles, 1, partner_at, *boxes)
+    radiate(6, 6, 1, 6, 48 - 32 * core, 80, *sent_out)
+    for side in range(2):
+
+        @pl.when(core == side)
+        def _(side=side):
+            inner = range(9) if side else range(3, 12)
+            move_fine(s["fine"], s["fine_g"], s["fine_in"], range(3, 9), inner, False)
+
+    for plane in range(2):
+
+        @pl.when(beside)
+        def _(plane=plane):
+            from_outer[plane].wait_recv()
+
+            @pl.when(above)
+            def _():
+                relay_above[plane].start()
+
+            @pl.when(below)
+            def _():
+                relay_below[plane].start()
+
     @pl.when(below)
     def _():
         for c in from_below:
@@ -454,24 +478,6 @@
         return 0
 
     lax.fori_loop(0, 2, ends, 0)
-    for plane in range(2):
-
-        @pl.when(beside)
-        def _(plane=plane):
-            from_outer[plane].wait_recv()
-
-            @pl.when(above)
-            def _():
-                relay_above[plane].start()
-
-            @pl.when(below)
-            def _():
-                relay_below[plane].start()
-
-    for c in to_partner:
-        c.wait()
-    arrange(tiles, 1, partner_at, *boxes)
-
     share = pltpu.make_async_remote_copy(
         src_ref=s["coarse"].at[:, :, 24:48, :],
         dst_ref=s["coarse"].at[:, :, pl.ds(pl.multiple_of(24 * outer_at, 8), 24), :],
@@ -480,7 +486,6 @@
         device_id=(box, partner),
         device_id_type=MESH,
     )
-    share.start()
 
     @pl.when(below)
     def _():
@@ -494,7 +499,8 @@
 
     arrange(tiles, 0, partner_at, *boxes)
     arrange(tiles, 2, partner_at, *boxes)
-    radiate(3, 12, 6, 48 - 32 * core, 80, *sent_out)
+    share.start()
+    radiate(3, 9, 2, 3, 48 - 32 * core, 80, *sent_out)
     near(1, False, *close)
     near(partner_at, True, *close)
     for side in range(2):
@@ -502,7 +508,8 @@
         @pl.when(core == side)
         def _(side=side):
             inner = range(9) if side else range(3, 12)
-            move_fine(s["fine"], s["fine_g"], s["fine_in"], inner, False)
+            lines = (0, 1, 2, 9, 10, 11)
+            move_fine(s["fine"], s["fine_g"], s["fine_in"], lines, inner, True)
 
     arrange(tiles, 1, outer_at, *boxes)
 
@@ -519,14 +526,14 @@
     arrange(tiles, 0, outer_at, *boxes)
     arrange(tiles, 2, outer_at, *boxes)
     lift(0, 9, outer_at, 1, *lifted)
-    radiate(3, 12, 12, 16 + 80 * core, 32, *sent_out)
+    radiate(3, 12, 1, 12, 16 + 80 * core, 32, *sent_out)
     near(outer_at, True, *close)
     for side in range(2):
 
         @pl.when(core == side)
         def _(side=side):
             outside = range(9, 12) if side else range(3)
-            move_fine(s["fine"], s["fine_g"], s["fine_in"], outside, True)
+            move_fine(s["fine"], s["fine_g"], s["fine_in"], range(12), outside, True)
 
     share.wait()
     move_coarse(s["coarse"], s["coarse_g"], s["coarse_in"])

time: 30.5 us -> 29 us (0.951)
  Pallas kernels: 28.8 us -> 27.3 us
    pallas_call x1, Pallas kernels: 28.8 us -> 27.3 us  [body(): pl.pallas_call(kernel, out_shape=jax.ShapeDtypeStruct((2, 6, 6, 4, 128),...]
where the time goes in v3:
time: 29 us; the launch traced here: 28.9 us
  Pallas kernels  27.3 us (94%)
  local copies, waits for them, and re-layouts  1.58 us (5%)
    pallas_call x1, Pallas kernels, body(): pl.pallas_call(kernel, out_shape=jax.ShapeDtypeStruct((2, 6, 6, 4, 128),...  27.3 us
    unnamed x1, local copies, waits for them, and re-layouts  1.58 us

profile of v3, /device:TPU:11, one launch (start us, length us, event | category | flops | bytes accessed | tf_op | source)
XLA Modules:
  0.0 28.9 jit_solution(10380142189323085843)
XLA Ops:
  0.0 27.3 %product.1 = f32[2,6,6,4,128]{4,3,2,1,0:T(4,128)} custom-call(f32[2,6,6,4,128]{4,3,2,1,0:T(4,128)} %bitcast.7, f32[2,512,128]{2,1,0:T(8,128)} %rad_ref.1, f32[1024,512]{1,0:T(8,128)} %interp_ref.1, f32[49,2,512]{2,1,0:T(2,128)} %bitcast.6, f32[49,2,1024]{2,1,0:T(2,128)} %bitcast.5, f32[4,1024]{1,0:T(4,128)} %ph_ref.1, f32[2,9,128,128]{3,2,1,0:T(8,128)} %nb_ref.1, ...), custom_call_target="tpu_custom_call" | custom-call | tf_op jit(solution)/shard_map/product/pallas_call | solution.py:562
  27.3 1.6 %copy.12 = f32[2,4,6,6,128]{4,1,3,2,0:T(4,128)} copy(f32[2,4,6,6,128]{4,1,3,2,0:T(4,128)} %bitcast.4) | data formatting | bytes 294912

commit v4 on v3

--- a/solution.py
+++ b/solution.py
@@ -120,12 +120,12 @@
             ]
 
 
-def move_coarse(coarse, coarse_g, coarse_in):
+def move_coarse(coarse, coarse_g, coarse_in, columns, add):
     def one(mt, _):
         plain = [None] * 9
         turned = [None] * 9
         for sx in range(9):
-            for sy in range(9):
+            for sy in columns:
                 value = None
                 for bx in range(3):
                     for by in range(3):
@@ -143,7 +143,12 @@
                         plain[b] = p if plain[b] is None else plain[b] + p
                         turned[b] = q if turned[b] is None else turned[b] + q
         for b in range(9):
-            coarse_in[mt, b * 8 : b * 8 + 8, :] = plain[b] + turn(turned[b])
+            if plain[b] is None:
+                continue
+            total = plain[b] + turn(turned[b])
+            if add:
+                total = total + coarse_in[mt, b * 8 : b * 8 + 8, :]
+            coarse_in[mt, b * 8 : b * 8 + 8, :] = total
         return 0
 
     lax.fori_loop(0, 8, one, 0)
@@ -456,6 +461,32 @@
             def _():
                 relay_below[plane].start()
 
+    @pl.when(above)
+    def _():
+        for c in from_above:
+            c.wait_recv()
+        for c in pass_high:
+            c.start()
+
+    arrange(tiles, 2, 1, *boxes)
+    lift(6, 3, 1, 1, *lifted)
+    arrange(tiles, 1, outer_at, *boxes)
+    lift(3, 3, outer_at, 1, *lifted)
+
+    @pl.when(above)
+    def _():
+        for c in pass_high:
+            c.wait()
+
+    arrange(tiles, 2, partner_at, *boxes)
+    radiate(12, 3, 1, 3, 48 - 32 * core, 80, *sent_out)
+    for side in range(2):
+
+        @pl.when(core == side)
+        def _(side=side):
+            inner = range(9) if side else range(3, 12)
+            move_fine(s["fine"], s["fine_g"], s["fine_in"], range(9, 12), inner, True)
+
     @pl.when(below)
     def _():
         for c in from_below:
@@ -463,21 +494,8 @@
         for c in pass_low:
             c.start()
 
-    @pl.when(above)
-    def _():
-        for c in from_above:
-            c.wait_recv()
-        for c in pass_high:
-            c.start()
-
     arrange(tiles, 0, 1, *boxes)
-    arrange(tiles, 2, 1, *boxes)
-
-    def ends(i, _):
-        lift(6 * i, 3, 1, 1, *lifted)
-        return 0
-
-    lax.fori_loop(0, 2, ends, 0)
+    lift(0, 3, 1, 1, *lifted)
     share = pltpu.make_async_remote_copy(
         src_ref=s["coarse"].at[:, :, 24:48, :],
         dst_ref=s["coarse"].at[:, :, pl.ds(pl.multiple_of(24 * outer_at, 8), 24), :],
@@ -492,15 +510,9 @@
         for c in pass_low:
             c.wait()
 
-    @pl.when(above)
-    def _():
-        for c in pass_high:
-            c.wait()
-
     arrange(tiles, 0, partner_at, *boxes)
-    arrange(tiles, 2, partner_at, *boxes)
     share.start()
-    radiate(3, 9, 2, 3, 48 - 32 * core, 80, *sent_out)
+    radiate(3, 3, 1, 3, 48 - 32 * core, 80, *sent_out)
     near(1, False, *close)
     near(partner_at, True, *close)
     for side in range(2):
@@ -508,10 +520,15 @@
         @pl.when(core == side)
         def _(side=side):
             inner = range(9) if side else range(3, 12)
-            lines = (0, 1, 2, 9, 10, 11)
-            move_fine(s["fine"], s["fine_g"], s["fine_in"], lines, inner, True)
-
-    arrange(tiles, 1, outer_at, *boxes)
+            move_fine(s["fine"], s["fine_g"], s["fine_in"], range(3), inner, True)
+
+    share.wait()
+    for side in range(2):
+
+        @pl.when(core == side)
+        def _(side=side):
+            inner = range(6) if side else range(3, 9)
+            move_coarse(s["coarse"], s["coarse_g"], s["coarse_in"], inner, False)
 
     @pl.when(jnp.logical_and(beside, below))
     def _():
@@ -525,7 +542,12 @@
 
     arrange(tiles, 0, outer_at, *boxes)
     arrange(tiles, 2, outer_at, *boxes)
-    lift(0, 9, outer_at, 1, *lifted)
+
+    def ends(i, _):
+        lift(6 * i, 3, outer_at, 1, *lifted)
+        return 0
+
+    lax.fori_loop(0, 2, ends, 0)
     radiate(3, 12, 1, 12, 16 + 80 * core, 32, *sent_out)
     near(outer_at, True, *close)
     for side in range(2):
@@ -534,9 +556,9 @@
         def _(side=side):
             outside = range(9, 12) if side else range(3)
             move_fine(s["fine"], s["fine_g"], s["fine_in"], range(12), outside, True)
-
-    share.wait()
-    move_coarse(s["coarse"], s["coarse_g"], s["coarse_in"])
+            outside = range(6, 9) if side else range(3)
+            move_coarse(s["coarse"], s["coarse_g"], s["coarse_in"], outside, True)
+
     lower(s["coarse_in"], s["wide_h"], s["wide_l"], s["cosine"], s["sine"], s["coarse_y"])
     finish(s["fine_in"], s["rad_h"], s["rad_l"], s["coarse_y"], s["near_y"], out_ref)
 

time: 29 us -> 28.8 us (level)
  Pallas kernels: 27.3 us -> 26.9 us
    pallas_call x1, Pallas kernels: 27.3 us -> 26.9 us  [body(): pl.pallas_call(kernel, out_shape=jax.ShapeDtypeStruct((2, 6, 6, 4, 128),...]
where the time goes in v4:
time: 28.8 us; the launch traced here: 28.5 us
  Pallas kernels  26.9 us (93%)
  local copies, waits for them, and re-layouts  1.58 us (5%)
    pallas_call x1, Pallas kernels, body(): pl.pallas_call(kernel, out_shape=jax.ShapeDtypeStruct((2, 6, 6, 4, 128),...  26.9 us
    unnamed x1, local copies, waits for them, and re-layouts  1.58 us

profile of v4, /device:TPU:11, one launch (start us, length us, event | category | flops | bytes accessed | tf_op | source)
XLA Modules:
  0.0 28.5 jit_solution(6840333618799446673)
XLA Ops:
  0.0 26.9 %product.1 = f32[2,6,6,4,128]{4,3,2,1,0:T(4,128)} custom-call(f32[2,6,6,4,128]{4,3,2,1,0:T(4,128)} %bitcast.7, f32[2,512,128]{2,1,0:T(8,128)} %rad_ref.1, f32[1024,512]{1,0:T(8,128)} %interp_ref.1, f32[49,2,512]{2,1,0:T(2,128)} %bitcast.6, f32[49,2,1024]{2,1,0:T(2,128)} %bitcast.5, f32[4,1024]{1,0:T(4,128)} %ph_ref.1, f32[2,9,128,128]{3,2,1,0:T(8,128)} %nb_ref.1, ...), custom_call_target="tpu_custom_call" | custom-call | tf_op jit(solution)/shard_map/product/pallas_call | solution.py:584
  26.9 1.6 %copy.12 = f32[2,4,6,6,128]{4,1,3,2,0:T(4,128)} copy(f32[2,4,6,6,128]{4,1,3,2,0:T(4,128)} %bitcast.4) | data formatting | bytes 294912

commit v5 on v3

--- a/solution.py
+++ b/solution.py
@@ -120,12 +120,12 @@
             ]
 
 
-def move_coarse(coarse, coarse_g, coarse_in):
+def move_coarse(coarse, coarse_g, coarse_in, columns, add):
     def one(mt, _):
         plain = [None] * 9
         turned = [None] * 9
         for sx in range(9):
-            for sy in range(9):
+            for sy in columns:
                 value = None
                 for bx in range(3):
                     for by in range(3):
@@ -143,7 +143,12 @@
                         plain[b] = p if plain[b] is None else plain[b] + p
                         turned[b] = q if turned[b] is None else turned[b] + q
         for b in range(9):
-            coarse_in[mt, b * 8 : b * 8 + 8, :] = plain[b] + turn(turned[b])
+            if plain[b] is None:
+                continue
+            total = plain[b] + turn(turned[b])
+            if add:
+                total = total + coarse_in[mt, b * 8 : b * 8 + 8, :]
+            coarse_in[mt, b * 8 : b * 8 + 8, :] = total
         return 0
 
     lax.fori_loop(0, 8, one, 0)
@@ -371,10 +376,7 @@
 
     own.wait()
 
-    lines_z = boxes_all // 2
-    late = jnp.logical_or(box % lines_z == 0, box % lines_z == lines_z - 1)
-
-    @pl.when(jnp.logical_and(beside, jnp.logical_not(late)))
+    @pl.when(beside)
     def _():
         for c in to_outer:
             c.start()
@@ -412,11 +414,6 @@
         s["tf"], s["tc"], s["ff"], s["fc"], s["nm"], s["fine_g"], s["coarse_g"], s["near_g"], s["listed"],
         col * 3,
     )
-
-    @pl.when(jnp.logical_and(beside, late))
-    def _():
-        for c in to_outer:
-            c.start()
 
     for name in ("phase", "rad", "interp", "blocks"):
         loads[name].wait()
@@ -511,6 +508,14 @@
             lines = (0, 1, 2, 9, 10, 11)
             move_fine(s["fine"], s["fine_g"], s["fine_in"], lines, inner, True)
 
+    share.wait()
+    for side in range(2):
+
+        @pl.when(core == side)
+        def _(side=side):
+            inner = range(6) if side else range(3, 9)
+            move_coarse(s["coarse"], s["coarse_g"], s["coarse_in"], inner, False)
+
     arrange(tiles, 1, outer_at, *boxes)
 
     @pl.when(jnp.logical_and(beside, below))
@@ -534,9 +539,9 @@
         def _(side=side):
             outside = range(9, 12) if side else range(3)
             move_fine(s["fine"], s["fine_g"], s["fine_in"], range(12), outside, True)
-
-    share.wait()
-    move_coarse(s["coarse"], s["coarse_g"], s["coarse_in"])
+            outside = range(6, 9) if side else range(3)
+            move_coarse(s["coarse"], s["coarse_g"], s["coarse_in"], outside, True)
+
     lower(s["coarse_in"], s["wide_h"], s["wide_l"], s["cosine"], s["sine"], s["coarse_y"])
     finish(s["fine_in"], s["rad_h"], s["rad_l"], s["coarse_y"], s["near_y"], out_ref)
 

time: 29 us -> 27.5 us (0.948)
  Pallas kernels: 27.3 us -> 25.8 us
    pallas_call x1, Pallas kernels: 27.3 us -> 25.8 us  [body(): pl.pallas_call(kernel, out_shape=jax.ShapeDtypeStruct((2, 6, 6, 4, 128),...]
where the time goes in v5:
time: 27.5 us; the launch traced here: 27.4 us
  Pallas kernels  25.8 us (94%)
  local copies, waits for them, and re-layouts  1.58 us (6%)
    pallas_call x1, Pallas kernels, body(): pl.pallas_call(kernel, out_shape=jax.ShapeDtypeStruct((2, 6, 6, 4, 128),...  25.8 us
    unnamed x1, local copies, waits for them, and re-layouts  1.58 us

profile of v5, /device:TPU:11, one launch (start us, length us, event | category | flops | bytes accessed | tf_op | source)
XLA Modules:
  0.0 27.4 jit_solution(12242598059953193143)
XLA Ops:
  0.0 25.8 %product.1 = f32[2,6,6,4,128]{4,3,2,1,0:T(4,128)} custom-call(f32[2,6,6,4,128]{4,3,2,1,0:T(4,128)} %bitcast.7, f32[2,512,128]{2,1,0:T(8,128)} %rad_ref.1, f32[1024,512]{1,0:T(8,128)} %interp_ref.1, f32[49,2,512]{2,1,0:T(2,128)} %bitcast.6, f32[49,2,1024]{2,1,0:T(2,128)} %bitcast.5, f32[4,1024]{1,0:T(4,128)} %ph_ref.1, f32[2,9,128,128]{3,2,1,0:T(8,128)} %nb_ref.1, ...), custom_call_target="tpu_custom_call" | custom-call | tf_op jit(solution)/shard_map/product/pallas_call | solution.py:567
  25.8 1.6 %copy.12 = f32[2,4,6,6,128]{4,1,3,2,0:T(4,128)} copy(f32[2,4,6,6,128]{4,1,3,2,0:T(4,128)} %bitcast.4) | data formatting | bytes 294912
